TPU v7x, 256 devices: a 2x2x32 block of a 4x8x32 slice. The times are simulated.
256 devices in a mesh: groups: 4 (over y, x), dp: 2 (over core), seq: 32 (over z).
Axes of the slice: x: 2, y: 2, z: 32, core: 2. Of those that a mesh axis runs over, the one named last changes fastest.
The devices are a block of a 4x8x32 slice.
Arguments:
- history: bfloat16 [16, 3072, 1024], P(('groups', 'dp'), 'seq'), parts along dimension 0, may hold values from -20 to 20
- candidates: bfloat16 [8, 2048, 1024], P(('groups', 'dp'), 'seq'), parts along dimension 0, may hold values from -6 to 6
- lengths: int32 [16], P(('groups', 'dp')), parts along dimension 0, may hold values from 384 to 3072
- assignment: int32 [8, 2048], P(('groups', 'dp'), 'seq'), parts along dimension 0, may hold values from 0 to 1, as said below
- weight_in: bfloat16 [1024, 4096], replicated, may hold values from -0.1875 to 0.1875
- weight_out: bfloat16 [1024, 1024], replicated, may hold values from -0.1875 to 0.1875
- gain_in: float32 [1024], replicated, may hold values from 0.25 to 1.75
- gain_attn: float32 [1024], replicated, may hold values from 0.25 to 1.75
Outputs:
- history_out: bfloat16 [16, 3072, 1024], P(('groups', 'dp'), 'seq'), parts along dimension 0
- candidate_out: bfloat16 [8, 2048, 1024], P(('groups', 'dp'), 'seq'), parts along dimension 0
There are 4 independent parts, one for each index of `groups`. A program takes and returns all parts, laid end to end along the dimension named above; an argument that names none is the same for every part. Nothing has to cross between parts.
Inputs may be any that keep to these rules, and one draw needn't show every extreme that they name: `assignment`: of the 64 candidates of one device, at most 40 belong to either history; in every dp index some device has exactly 40 of the first and another exactly 40 of the second.
All inputs are finite; a program needn't handle non-finite values.
Results may differ from a plain program's by a relative error of at most 0.0075.
Values may be sent and summed in bfloat16 or wider, within the bound.
A program may use at most 192 MiB of HBM per device.

v0:
```python
import functools

import jax
import jax.numpy as jnp
from jax import lax
from jax.experimental import pallas as pl
from jax.experimental.pallas import tpu as pltpu
from jax.sharding import PartitionSpec as P

H = 16
HD = 64
PAIR = 2 * HD
EPS = 1e-06
MESH = pl.DeviceIdType.MESH


def normed_rows(rows, gain):
    rows = rows.astype(jnp.float32)
    mean = jnp.mean(rows * rows, axis=-1, keepdims=True)
    return rows * lax.rsqrt(mean + EPS) * gain


def layer_kernel(
    ring,
    hist_hbm,
    cand_hbm,
    len_ref,
    assign_ref,
    w_in_hbm,
    w_out_hbm,
    gain_in_ref,
    gain_attn_ref,
    hist_out,
    cand_out,
    slots,
    own,
    cand,
    w_in,
    w_out,
    xn,
    gate,
    qz,
    kv,
    acc,
    lim,
    mask,
    load_sem,
    send_sem,
    recv_sem,
):
    hist_local, tok, width = own.shape
    cands = cand.shape[0]
    rows = tok + cands
    pairs = width // PAIR
    hist_rows = hist_local * tok
    half = ring // 2
    me = lax.axis_index("seq")
    right, left = lax.rem(me + 1, ring), lax.rem(me + ring - 1, ring)
    towards = (right, left)

    def send(src, slot, member, way):
        number = hist_local * slot + member
        return pltpu.make_async_remote_copy(
            src_ref=src,
            dst_ref=slots.at[slot, member, way],
            send_sem=send_sem.at[way, number],
            recv_sem=recv_sem.at[way, number],
            device_id={"seq": towards[way]},
            device_id_type=MESH,
        )

    loads = (
        pltpu.make_async_copy(hist_hbm, own, load_sem.at[0]),
        pltpu.make_async_copy(cand_hbm, cand, load_sem.at[1]),
        pltpu.make_async_copy(w_in_hbm, w_in, load_sem.at[2]),
        pltpu.make_async_copy(w_out_hbm, w_out, load_sem.at[3]),
    )
    for load in loads:
        load.start()

    barrier = pltpu.get_barrier_semaphore()
    for neighbour in towards:
        pl.semaphore_signal(barrier, inc=1, device_id={"seq": neighbour}, device_id_type=MESH)
    pl.semaphore_wait(barrier, 2)
    for member in range(hist_local):
        for way in range(2):
            send(hist_hbm.at[member], 0, member, way).start()

    gain_in = gain_in_ref[...]

    row_of = lax.broadcasted_iota(jnp.int32, (tok, 2 * PAIR), 0)
    eye = lax.broadcasted_iota(jnp.int32, (cands, cands), 0) == lax.broadcasted_iota(
        jnp.int32, (cands, cands), 1
    )
    owner = jnp.sum(
        jnp.where(eye, jnp.broadcast_to(assign_ref[...].astype(jnp.float32), (cands, cands)), 0.0),
        axis=1,
        keepdims=True,
    )
    for member in range(hist_local):
        valid = len_ref[member]
        lim[member, :tok, :] = jnp.minimum(me * tok + row_of + 1, valid).astype(jnp.float32)
        mine = jnp.where(owner == float(member), 1.0, 0.0)
        lim[member, tok:, :] = jnp.broadcast_to(mine, (cands, 2 * PAIR)) * valid.astype(jnp.float32)

    for load in loads[:3]:
        load.wait()
    for member in range(hist_local):
        xn[member * tok : (member + 1) * tok, :] = normed_rows(own[member], gain_in).astype(
            jnp.bfloat16
        )
    xn[hist_rows:, :] = normed_rows(cand[...], gain_in).astype(jnp.bfloat16)
    lane = lax.broadcasted_iota(jnp.int32, (1, PAIR), 1)
    first_head = lane < HD
    for block in range(width // 256):
        cols = slice(block * 256, (block + 1) * 256)
        part = 0.5 * jnp.dot(xn[...], w_in[:, cols], preferred_element_type=jnp.float32)
        gate[:, cols] = (part * (1.0 + jnp.tanh(part))).astype(jnp.bfloat16)
    for block in range(width // 256):
        cols = slice(width + block * 256, width + (block + 1) * 256)
        query = jnp.dot(xn[...], w_in[:, cols], preferred_element_type=jnp.float32)
        query = query.astype(jnp.bfloat16).astype(jnp.float32) * (0.5 * HD ** (-0.5))
        for inner in range(2):
            two = query[:, inner * PAIR : (inner + 1) * PAIR]
            for head in range(2):
                keep = jnp.where(first_head == (head == 0), two, 0.0).astype(jnp.bfloat16)
                for member in range(hist_local):
                    at = head * rows
                    qz[member, 2 * block + inner, at : at + tok, :] = keep[
                        member * tok : (member + 1) * tok
                    ]
                    qz[member, 2 * block + inner, at + tok : at + rows, :] = keep[hist_rows:]

    def project_keys():
        for block in range(2 * width // 256):
            start = 2 * width + block * 256
            part = jnp.dot(
                xn[:hist_rows, :], w_in[:, start : start + 256], preferred_element_type=jnp.float32
            ).astype(jnp.bfloat16)
            kv[2 * block] = part[:, :PAIR]
            kv[2 * block + 1] = part[:, PAIR:]

    def attend(member, key_rows, count, positions, fresh):
        mask[:, :count] = jnp.where(positions < lim[member, :, :count], 1.0, 0.0)
        for pair in range(pairs):
            half_score = lax.dot_general(
                qz[member, pair],
                kv[pair, key_rows, :],
                (((1,), (1,)), ((), ())),
                preferred_element_type=jnp.float32,
            )
            weights = []
            for head in range(2):
                part = half_score[head * rows : (head + 1) * rows]
                weights.append(
                    (part * mask[:, :count] * (1.0 + jnp.tanh(part))).astype(jnp.bfloat16)
                )
            values = kv[pairs + pair, key_rows, :]
            first = jnp.dot(weights[0], values, preferred_element_type=jnp.float32)
            second = jnp.dot(weights[1], values, preferred_element_type=jnp.float32)
            both = jnp.where(first_head, first, second)
            if fresh:
                acc[member, pair] = both
            else:
                acc[member, pair] += both

    def place_of(block, count):
        inside = lax.broadcasted_iota(jnp.int32, (1, count), 1)
        return (block * tok + inside).astype(jnp.float32)

    project_keys()
    for member in range(hist_local):
        attend(member, slice(member * tok, (member + 1) * tok), tok, place_of(me, tok), True)

    @pl.loop(0, hist_local * (half - 1))
    def _(number):
        step, member = number // hist_local, lax.rem(number, hist_local)
        for way in range(2):
            send(slots.at[step, member, way], step, member, way).wait_recv()

            @pl.when((step < half - 2) | (member == way))
            def _():
                send(slots.at[step, member, way], step + 1, member, way).start()

        for way in range(2):
            xn[way * tok : (way + 1) * tok, :] = normed_rows(
                slots[step, member, way], gain_in
            ).astype(jnp.bfloat16)
        project_keys()
        from_left = lax.rem(me + ring - 1 - step, ring)
        from_right = lax.rem(me + 1 + step, ring)
        inside = lax.broadcasted_iota(jnp.int32, (1, 2 * tok), 1)
        positions = jnp.where(
            inside < tok, from_left * tok + inside, (from_right - 1) * tok + inside
        ).astype(jnp.float32)
        attend(member, slice(0, 2 * tok), 2 * tok, positions, False)

    opposite = lax.rem(me + half, ring)
    for member in range(hist_local):
        send(slots.at[half - 1, member, member], half - 1, member, member).wait_recv()
        xn[member * tok : (member + 1) * tok, :] = normed_rows(
            slots[half - 1, member, member], gain_in
        ).astype(jnp.bfloat16)
    project_keys()
    for member in range(hist_local):
        attend(
            member, slice(member * tok, (member + 1) * tok), tok, place_of(opposite, tok), False
        )

    loads[3].wait()
    gain_attn = gain_attn_ref[...]

    def finish(attended, gates, residual):
        attended = attended.astype(jnp.bfloat16)
        gated = (normed_rows(attended, gain_attn) * gates.astype(jnp.float32)).astype(jnp.bfloat16)
        outs = jnp.dot(gated, w_out[...], preferred_element_type=jnp.float32)
        return (residual.astype(jnp.float32) + outs).astype(jnp.bfloat16)

    for member in range(hist_local):
        attended = jnp.concatenate([acc[member, pair, :tok, :] for pair in range(pairs)], axis=1)
        hist_out[member] = finish(
            attended, gate[member * tok : (member + 1) * tok, :], own[member]
        )
    crossed = jnp.concatenate(
        [
            sum(acc[member, pair, tok:, :] for member in range(hist_local))
            for pair in range(pairs)
        ],
        axis=1,
    )
    cand_out[...] = finish(crossed, gate[hist_rows:, :], cand[...])

    @pl.loop(0, hist_local * (half - 1))
    def _(number):
        step, member = number // hist_local, lax.rem(number, hist_local)
        for way in range(2):
            send(slots.at[step, member, way], step, member, way).wait_send()

    for member in range(hist_local):
        send(slots.at[half - 1, member, member], half - 1, member, member).wait_send()


def per_device(history, candidates, lengths, assignment, weight_in, weight_out, gain_in, gain_attn):
    ring = lax.axis_size("seq")
    hist_local, tok, width = history.shape
    cands = candidates.shape[1]
    rows = tok + cands
    pairs = width // PAIR
    half = ring // 2
    whole = pl.BlockSpec(memory_space=pltpu.VMEM)
    scalars = pl.BlockSpec(memory_space=pltpu.SMEM)
    there = pl.BlockSpec(memory_space=pl.ANY)
    history_out, candidate_out = pl.pallas_call(
        functools.partial(layer_kernel, ring),
        out_shape=(
            jax.ShapeDtypeStruct(history.shape, jnp.bfloat16),
            jax.ShapeDtypeStruct((cands, width), jnp.bfloat16),
        ),
        in_specs=[there, there, scalars, whole, there, there, whole, whole],
        out_specs=(whole, whole),
        scratch_shapes=[
            pltpu.VMEM((half, hist_local, 2, tok, width), jnp.bfloat16),
            pltpu.VMEM((hist_local, tok, width), jnp.bfloat16),
            pltpu.VMEM((cands, width), jnp.bfloat16),
            pltpu.VMEM(weight_in.shape, jnp.bfloat16),
            pltpu.VMEM(weight_out.shape, jnp.bfloat16),
            pltpu.VMEM((hist_local * tok + cands, width), jnp.bfloat16),
            pltpu.VMEM((hist_local * tok + cands, width), jnp.bfloat16),
            pltpu.VMEM((hist_local, pairs, 2 * rows, PAIR), jnp.bfloat16),
            pltpu.VMEM((2 * pairs, 2 * tok, PAIR), jnp.bfloat16),
            pltpu.VMEM((hist_local, pairs, rows, PAIR), jnp.float32),
            pltpu.VMEM((hist_local, rows, 2 * PAIR), jnp.float32),
            pltpu.VMEM((rows, 2 * PAIR), jnp.float32),
            pltpu.SemaphoreType.DMA((4,)),
            pltpu.SemaphoreType.DMA((2, hist_local * half)),
            pltpu.SemaphoreType.DMA((2, hist_local * half)),
        ],
        compiler_params=pltpu.CompilerParams(
            collective_id=0, has_side_effects=True, vmem_limit_bytes=60 * 1024 * 1024
        ),
    )(
        history,
        candidates[0],
        lengths,
        assignment,
        weight_in,
        weight_out,
        gain_in.reshape(1, width),
        gain_attn.reshape(1, width),
    )
    return history_out, candidate_out[None]


def solution(mesh):
    in_specs = (
        P(("groups", "dp"), "seq", None),
        P(("groups", "dp"), "seq", None),
        P(("groups", "dp")),
        P(("groups", "dp"), "seq"),
        P(),
        P(),
        P(),
        P(),
    )
    out_specs = (P(("groups", "dp"), "seq", None), P(("groups", "dp"), "seq", None))
    return jax.shard_map(
        per_device, mesh=mesh, in_specs=in_specs, out_specs=out_specs, check_vma=False
    )
```

profile of v0, /device:TPU:46, one launch (start us, length us, event | category | flops | bytes accessed | tf_op | source)
XLA Modules:
  0.0 167.3 jit_solution(9589631785352681122)
XLA Ops:
  0.6 163.3 %shard_map.95 = (bf16[2,96,1024]{2,1,0:T(8,128)(2,1)}, bf16[64,1024]{1,0:T(8,128)(2,1)}) custom-call(bf16[2,96,1024]{2,1,0:T(8,128)(2,1)} %hist_hbm.1, bf16[64,1024]{1,0:T(8,128)(2,1)} %bitcast.4, s32[2]{0:T(128)} %len_ref.1, s32[1,64]{1,0:T(1,128)} %assign_ref.1, bf16[1024,4096]{1,0:T(8,128)(2,1)} %w_in_hbm.1, bf16[1024,1024]{1,0:T(8,128)(2,1)} %w_out_hbm.1, ...), custom_call_target="tpu_custom_call" | custom-call | tf_op jit(solution)/shard_map/pallas_call | solution.py:253
  163.9 1.8 %copy.12 = bf16[2,96,1024]{2,1,0:T(8,128)(2,1)} copy(bf16[2,96,1024]{2,1,0:T(8,128)(2,1)} %get-tuple-element.8) | data formatting | bytes 786432
  165.7 1.6 copy.13
where the time goes:
time: 167 us
  Pallas kernels  163 us (98%)
  local copies, waits for them, and re-layouts  3.33 us (2%)
    pallas_call x1, Pallas kernels, per_device(): pl.pallas_call(functools.partial(layer_kernel, ring), out_shape=(jax.Shap...  163 us

commit v1 on v0

v1 whole, which is shorter than its diff:
```python
import functools

import jax
import jax.numpy as jnp
from jax import lax
from jax.experimental import pallas as pl
from jax.experimental.pallas import tpu as pltpu
from jax.sharding import PartitionSpec as P

HD = 64
PAIR = 2 * HD
EPS = 1e-06
MESH = pl.DeviceIdType.MESH
MOST_EXTRA = 2


def normed_rows(rows, gain):
    rows = rows.astype(jnp.float32)
    mean = jnp.mean(rows * rows, axis=-1, keepdims=True)
    return rows * lax.rsqrt(mean + EPS) * gain


def lead_of(place):
    return jnp.maximum(2 * MOST_EXTRA + 1 - place, 0) * jnp.minimum(place, 1)


def late_of(place):
    return MOST_EXTRA * jnp.maximum(1 - place, 0)


def extra_of(place):
    return lax.div(lead_of(place), 2) + late_of(place)


def attend_kernel(
    ring,
    hist_hbm,
    cand_hbm,
    len_ref,
    assign_ref,
    w_in_hbm,
    gain_in_ref,
    gain_attn_ref,
    gated_out,
    from_left,
    from_right,
    own,
    cand,
    w_in,
    xn,
    gate,
    qz,
    kv,
    acc,
    lim,
    mask,
    load_sem,
    right_send,
    right_recv,
    left_send,
    left_recv,
):
    hist_local, tok, width = own.shape
    cands = cand.shape[0]
    rows = tok + cands
    pairs = width // PAIR
    hist_rows = hist_local * tok
    base = ring - 1
    me = lax.axis_index("seq")
    right, left = lax.rem(me + 1, ring), lax.rem(me + ring - 1, ring)
    lead, late, extra = lead_of(me), late_of(me), extra_of(me)
    early = extra - late
    turns = base - extra
    count_right = base - extra_of(right)
    count_left = base + extra_of(left)

    def send_right(src, chunk):
        return pltpu.make_async_remote_copy(
            src_ref=src,
            dst_ref=from_left.at[chunk],
            send_sem=right_send.at[chunk],
            recv_sem=right_recv.at[chunk],
            device_id={"seq": right},
            device_id_type=MESH,
        )

    def send_left(src, chunk):
        return pltpu.make_async_remote_copy(
            src_ref=src,
            dst_ref=from_right.at[chunk],
            send_sem=left_send.at[chunk],
            recv_sem=left_recv.at[chunk],
            device_id={"seq": left},
            device_id_type=MESH,
        )

    def pass_right(chunk):
        send_right(from_left.at[chunk], chunk).wait_recv()

        @pl.when(chunk + 2 < count_right)
        def _():
            send_right(from_left.at[chunk], chunk + 2).start()

    def pass_left(chunk):
        send_left(from_right.at[chunk], chunk).wait_recv()

        @pl.when(chunk + 2 < count_left)
        def _():
            send_left(from_right.at[chunk], chunk + 2).start()

    barrier = pltpu.get_barrier_semaphore()
    for neighbour in (right, left):
        pl.semaphore_signal(barrier, inc=1, device_id={"seq": neighbour}, device_id_type=MESH)
    loads = (
        pltpu.make_async_copy(hist_hbm, own, load_sem.at[0]),
        pltpu.make_async_copy(cand_hbm, cand, load_sem.at[1]),
        pltpu.make_async_copy(w_in_hbm, w_in, load_sem.at[2]),
    )
    for load in loads:
        load.start()
    pl.semaphore_wait(barrier, 2)
    loads[0].wait()
    for chunk in range(hist_local):
        send_right(own.at[chunk], chunk).start()
        send_left(own.at[hist_local - 1 - chunk], chunk).start()

    gain_in = gain_in_ref[...]
    lane = lax.broadcasted_iota(jnp.int32, (1, PAIR), 1)
    first_head = lane < HD

    def project_keys():
        for block in range(2 * width // 256):
            start = 2 * width + block * 256
            part = jnp.dot(
                xn[:hist_rows, :], w_in[:, start : start + 256], preferred_element_type=jnp.float32
            ).astype(jnp.bfloat16)
            kv[2 * block] = part[:, :PAIR]
            kv[2 * block + 1] = part[:, PAIR:]

    def attend_rows(member, side, block, first_row, last_row, fresh):
        key_rows = slice(side * tok, (side + 1) * tok)
        count = last_row - first_row
        positions = block * tok + lax.broadcasted_iota(jnp.int32, (1, tok), 1)
        mask[first_row:last_row, :tok] = jnp.where(
            positions.astype(jnp.float32) < lim[member, first_row:last_row, :tok], 1.0, 0.0
        )
        for pair in range(pairs):
            half_score = lax.dot_general(
                qz[member, pair, 2 * first_row : 2 * last_row, :],
                kv[pair, key_rows, :],
                (((1,), (1,)), ((), ())),
                preferred_element_type=jnp.float32,
            )
            values = kv[pairs + pair, key_rows, :]
            parts = []
            for head in range(2):
                part = half_score[head * count : (head + 1) * count]
                weights = part * mask[first_row:last_row, :tok] * (1.0 + jnp.tanh(part))
                parts.append(
                    jnp.dot(
                        weights.astype(jnp.bfloat16), values, preferred_element_type=jnp.float32
                    )
                )
            both = jnp.where(first_head, parts[0], parts[1])
            if fresh:
                acc[member, pair, first_row:last_row, :] = both
            else:
                acc[member, pair, first_row:last_row, :] += both

    def attend(member, side, block):
        attend_rows(member, side, block, tok, rows, False)

        @pl.when(block < me)
        def _():
            attend_rows(member, side, block, 0, tok, False)

    row_of = lax.broadcasted_iota(jnp.int32, (tok, PAIR), 0)
    eye = lax.broadcasted_iota(jnp.int32, (cands, cands), 0) == lax.broadcasted_iota(
        jnp.int32, (cands, cands), 1
    )
    owners = jnp.broadcast_to(assign_ref[...].astype(jnp.float32), (cands, cands))
    owner = jnp.sum(jnp.where(eye, owners, 0.0), axis=1, keepdims=True)
    for member in range(hist_local):
        valid = len_ref[member]
        lim[member, :tok, :] = jnp.minimum(me * tok + row_of + 1, valid).astype(jnp.float32)
        mine = jnp.where(owner == float(member), 1.0, 0.0)
        lim[member, tok:, :] = jnp.broadcast_to(mine, (cands, PAIR)) * valid.astype(
            jnp.float32
        )

    for member in range(hist_local):
        xn[member * tok : (member + 1) * tok, :] = normed_rows(own[member], gain_in).astype(
            jnp.bfloat16
        )
    loads[1].wait()
    xn[hist_rows:, :] = normed_rows(cand[...], gain_in).astype(jnp.bfloat16)
    loads[2].wait()
    for block in range(width // 256):
        cols = slice(block * 256, (block + 1) * 256)
        part = 0.5 * jnp.dot(xn[...], w_in[:, cols], preferred_element_type=jnp.float32)
        gate[:, cols] = (part * (1.0 + jnp.tanh(part))).astype(jnp.bfloat16)
    for block in range(width // 256):
        cols = slice(width + block * 256, width + (block + 1) * 256)
        query = jnp.dot(xn[...], w_in[:, cols], preferred_element_type=jnp.float32)
        query = query.astype(jnp.bfloat16).astype(jnp.float32) * (0.5 * HD ** (-0.5))
        for inner in range(2):
            two = query[:, inner * PAIR : (inner + 1) * PAIR]
            for head in range(2):
                keep = jnp.where(first_head == (head == 0), two, 0.0).astype(jnp.bfloat16)
                for member in range(hist_local):
                    at = head * tok
                    qz[member, 2 * block + inner, at : at + tok, :] = keep[
                        member * tok : (member + 1) * tok
                    ]
                    at = 2 * tok + head * cands
                    qz[member, 2 * block + inner, at : at + cands, :] = keep[hist_rows:]
    project_keys()
    for member in range(hist_local):
        attend_rows(member, member, me, tok, rows, True)
        attend_rows(member, member, me, 0, tok, True)

    def unit(first, first_member, first_block, second, second_member, second_block):
        for side, chunk in enumerate((first, second)):
            xn[side * tok : (side + 1) * tok, :] = normed_rows(chunk[...], gain_in).astype(
                jnp.bfloat16
            )
        project_keys()
        attend(first_member, 0, first_block)
        attend(second_member, 1, second_block)

    def block_right(chunk):
        return lax.rem(me + 1 + lax.div(chunk, 2), ring)

    @pl.loop(0, lead)
    def _(chunk):
        pass_left(chunk)

    @pl.loop(0, turns)
    def _(turn):
        @pl.when(turn + lead < base + extra)
        def _():
            pass_left(turn + lead)

        pass_right(turn)
        other = turn + 2 * jnp.minimum(early, lax.div(jnp.maximum(turn - 1, 0), 2))
        member = lax.rem(turn, 2)
        unit(
            from_left.at[turn],
            member,
            lax.rem(me + ring - 1 - lax.div(turn, 2), ring),
            from_right.at[other],
            lax.rem(other + 1, 2),
            block_right(other),
        )

        due_late = (late > 0) & ((turn == turns - 4) | (turn == turns - 2))
        due_early = ((early > 0) & (turn == 2)) | ((early > 1) & (turn == 4))
        chunk = turn + 2 * late + (turn - 1) * jnp.minimum(me, 1)

        @pl.when(due_late)
        def _():
            pass_left(chunk)
            pass_left(chunk + 1)

        @pl.when(due_late | due_early)
        def _():
            unit(
                from_right.at[chunk],
                lax.rem(chunk + 1, 2),
                block_right(chunk),
                from_right.at[chunk + 1],
                lax.rem(chunk, 2),
                block_right(chunk + 1),
            )

    gain_attn = gain_attn_ref[...]

    def gated(attended, gates):
        attended = attended.astype(jnp.bfloat16)
        return (normed_rows(attended, gain_attn) * gates.astype(jnp.float32)).astype(jnp.bfloat16)

    for member in range(hist_local):
        mine = slice(member * tok, (member + 1) * tok)
        attended = jnp.concatenate([acc[member, pair, :tok, :] for pair in range(pairs)], axis=1)
        gated_out[mine, :] = gated(attended, gate[mine, :])
    crossed = jnp.concatenate(
        [
            sum(acc[member, pair, tok:, :] for member in range(hist_local))
            for pair in range(pairs)
        ],
        axis=1,
    )
    gated_out[hist_rows:, :] = gated(crossed, gate[hist_rows:, :])

    @pl.loop(0, count_right)
    def _(chunk):
        send_right(own.at[0], chunk).wait_send()

    @pl.loop(0, count_left)
    def _(chunk):
        send_left(own.at[0], chunk).wait_send()


def output_kernel(gated, w_out, history, candidates, history_out, candidate_out):
    hist_local, tok, width = history.shape
    hist_rows = hist_local * tok
    for block in range(width // 256):
        cols = slice(block * 256, (block + 1) * 256)
        outs = jnp.dot(gated[...], w_out[:, cols], preferred_element_type=jnp.float32)
        for member in range(hist_local):
            history_out[member, :, cols] = (
                history[member, :, cols].astype(jnp.float32)
                + outs[member * tok : (member + 1) * tok]
            ).astype(jnp.bfloat16)
        candidate_out[:, cols] = (
            candidates[:, cols].astype(jnp.float32) + outs[hist_rows:]
        ).astype(jnp.bfloat16)


def per_device(history, candidates, lengths, assignment, weight_in, weight_out, gain_in, gain_attn):
    ring = lax.axis_size("seq")
    hist_local, tok, width = history.shape
    cands = candidates.shape[1]
    rows = tok + cands
    all_rows = hist_local * tok + cands
    pairs = width // PAIR
    whole = pl.BlockSpec(memory_space=pltpu.VMEM)
    scalars = pl.BlockSpec(memory_space=pltpu.SMEM)
    there = pl.BlockSpec(memory_space=pltpu.HBM)
    gated = pl.pallas_call(
        functools.partial(attend_kernel, ring),
        out_shape=jax.ShapeDtypeStruct((all_rows, width), jnp.bfloat16),
        in_specs=[there, there, scalars, whole, there, whole, whole],
        out_specs=whole,
        scratch_shapes=[
            pltpu.VMEM((ring - 1, tok, width), jnp.bfloat16),
            pltpu.VMEM((ring - 1 + MOST_EXTRA, tok, width), jnp.bfloat16),
            pltpu.VMEM((hist_local, tok, width), jnp.bfloat16),
            pltpu.VMEM((cands, width), jnp.bfloat16),
            pltpu.VMEM(weight_in.shape, jnp.bfloat16),
            pltpu.VMEM((all_rows, width), jnp.bfloat16),
            pltpu.VMEM((all_rows, width), jnp.bfloat16),
            pltpu.VMEM((hist_local, pairs, 2 * rows, PAIR), jnp.bfloat16),
            pltpu.VMEM((2 * pairs, hist_local * tok, PAIR), jnp.bfloat16),
            pltpu.VMEM((hist_local, pairs, rows, PAIR), jnp.float32),
            pltpu.VMEM((hist_local, rows, PAIR), jnp.float32),
            pltpu.VMEM((rows, PAIR), jnp.float32),
            pltpu.SemaphoreType.DMA((3,)),
            pltpu.SemaphoreType.DMA((ring - 1,)),
            pltpu.SemaphoreType.DMA((ring - 1,)),
            pltpu.SemaphoreType.DMA((ring - 1 + MOST_EXTRA,)),
            pltpu.SemaphoreType.DMA((ring - 1 + MOST_EXTRA,)),
        ],
        compiler_params=pltpu.CompilerParams(
            collective_id=0, has_side_effects=True, vmem_limit_bytes=58 * 1024 * 1024
        ),
    )(
        history,
        candidates[0],
        lengths,
        assignment,
        weight_in,
        gain_in.reshape(1, width),
        gain_attn.reshape(1, width),
    )
    history_out, candidate_out = pl.pallas_call(
        output_kernel,
        out_shape=(
            jax.ShapeDtypeStruct(history.shape, jnp.bfloat16),
            jax.ShapeDtypeStruct((cands, width), jnp.bfloat16),
        ),
        in_specs=[whole, whole, whole, whole],
        out_specs=(whole, whole),
        compiler_params=pltpu.CompilerParams(vmem_limit_bytes=8 * 1024 * 1024),
    )(gated, weight_out, history, candidates[0])
    return history_out, candidate_out[None]


def solution(mesh):
    in_specs = (
        P(("groups", "dp"), "seq", None),
        P(("groups", "dp"), "seq", None),
        P(("groups", "dp")),
        P(("groups", "dp"), "seq"),
        P(),
        P(),
        P(),
        P(),
    )
    out_specs = (P(("groups", "dp"), "seq", None), P(("groups", "dp"), "seq", None))
    return jax.shard_map(
        per_device, mesh=mesh, in_specs=in_specs, out_specs=out_specs, check_vma=False
    )
```

time: 167 us -> 161 us (0.964)
  Pallas kernels: 163 us -> 158 us
  local copies, waits for them, and re-layouts: 3.33 us -> 1.05 us
    pallas_call x1 -> x2, Pallas kernels: 163 us -> 158 us  [the longest x1 157 us: per_device(): pl.pallas_call(functools.partial(attend_kernel, ring), out_shape=jax.Shap...]
    unnamed x2 -> x8, local copies, waits for them, and re-layouts: 3.33 us -> 1.05 us
where the time goes in v1:
time: 161 us; the launch traced here: 160 us
  Pallas kernels  158 us (98%)
    pallas_call x1, Pallas kernels, per_device(): pl.pallas_call(functools.partial(attend_kernel, ring), out_shape=jax.Shap...  157 us

profile of v1, /device:TPU:46, one launch (start us, length us, event | category | flops | bytes accessed | tf_op | source)
XLA Modules:
  0.0 159.9 jit_solution(11044835379912695337)
XLA Ops:
  0.6 0.0 copy-start.2
  0.6 0.0 copy-start
  0.7 0.0 copy-start.3
  0.7 156.7 %shard_map.95.gated = bf16[256,1024]{1,0:T(8,128)(2,1)} custom-call(bf16[2,96,1024]{2,1,0:T(8,128)(2,1)} %history.1, bf16[64,1024]{1,0:T(8,128)(2,1)} %bitcast.4, s32[2]{0:T(128)} %len_ref.1, s32[1,64]{1,0:T(1,128)} %assign_ref.1, bf16[1024,4096]{1,0:T(8,128)(2,1)} %w_in_hbm.1, f32[1,1024]{1,0:T(1,128)} %bitcast.6, f32[1,1024]{1,0:T(1,128)} %bitcast.7), custom_call_target="tpu_custom_call" | custom-call | tf_op jit(solution)/shard_map/pallas_call | solution.py:330
  157.4 0.0 copy-done.2
  157.4 0.0 copy-done
  157.4 0.0 copy-done.3
  157.4 0.0 copy-start.1
  157.4 1.0 copy-done.1
  158.4 1.5 shard_map.96
Async XLA Ops:
  0.6 156.7 %copy-start.2 = (bf16[2,96,1024]{2,1,0:T(8,128)(2,1)S(1)}, bf16[2,96,1024]{2,1,0:T(8,128)(2,1)}, u32[]{:S(2)}) copy-start(bf16[2,96,1024]{2,1,0:T(8,128)(2,1)} %history.1) | copy-start | bytes 1179652
  0.6 156.7 %copy-start = (bf16[1024,1024]{1,0:T(8,128)(2,1)S(1)}, bf16[1024,1024]{1,0:T(8,128)(2,1)}, u32[]{:S(2)}) copy-start(bf16[1024,1024]{1,0:T(8,128)(2,1)} %w_out.1) | copy-start | bytes 6291460
  0.7 156.7 %copy-start.3 = (bf16[1,64,1024]{2,1,0:T(8,128)(2,1)S(1)}, bf16[1,64,1024]{2,1,0:T(8,128)(2,1)}, u32[]{:S(2)}) copy-start(bf16[1,64,1024]{2,1,0:T(8,128)(2,1)} %param.9) | copy-start | bytes 393220
  157.4 1.0 copy-start.1

commit v2 on v1

--- a/solution.py
+++ b/solution.py
@@ -28,25 +28,33 @@
     return MOST_EXTRA * jnp.maximum(1 - place, 0)
 
 
-def extra_of(place):
-    return lax.div(lead_of(place), 2) + late_of(place)
+def back_of(place, ring):
+    return jnp.maximum(place + 2 - ring, 0)
+
+
+def extra_of(place, ring):
+    return lax.div(lead_of(place), 2) + late_of(place) - back_of(place, ring)
 
 
 def attend_kernel(
     ring,
     hist_hbm,
     cand_hbm,
+    len_hbm,
+    assign_hbm,
+    w_in_hbm,
+    gain_in_hbm,
+    gain_attn_hbm,
+    gated_hbm,
+    slots,
+    own,
+    cand,
     len_ref,
     assign_ref,
-    w_in_hbm,
+    w_in,
     gain_in_ref,
     gain_attn_ref,
-    gated_out,
-    from_left,
-    from_right,
-    own,
-    cand,
-    w_in,
+    gated_rows,
     xn,
     gate,
     qz,
@@ -55,6 +63,7 @@
     lim,
     mask,
     load_sem,
+    store_sem,
     right_send,
     right_recv,
     left_send,
@@ -68,16 +77,17 @@
     base = ring - 1
     me = lax.axis_index("seq")
     right, left = lax.rem(me + 1, ring), lax.rem(me + ring - 1, ring)
-    lead, late, extra = lead_of(me), late_of(me), extra_of(me)
-    early = extra - late
-    turns = base - extra
-    count_right = base - extra_of(right)
-    count_left = base + extra_of(left)
+    lead, late, back, extra = lead_of(me), late_of(me), back_of(me, ring), extra_of(me, ring)
+    early = lax.div(lead, 2)
+    turns = base - early - late - back
+    count_right = base - extra_of(right, ring)
+    count_left = base + extra_of(left, ring)
+    offset = base + MOST_EXTRA
 
     def send_right(src, chunk):
         return pltpu.make_async_remote_copy(
             src_ref=src,
-            dst_ref=from_left.at[chunk],
+            dst_ref=slots.at[chunk],
             send_sem=right_send.at[chunk],
             recv_sem=right_recv.at[chunk],
             device_id={"seq": right},
@@ -87,7 +97,7 @@
     def send_left(src, chunk):
         return pltpu.make_async_remote_copy(
             src_ref=src,
-            dst_ref=from_right.at[chunk],
+            dst_ref=slots.at[offset + chunk],
             send_sem=left_send.at[chunk],
             recv_sem=left_recv.at[chunk],
             device_id={"seq": left},
@@ -95,18 +105,18 @@
         )
 
     def pass_right(chunk):
-        send_right(from_left.at[chunk], chunk).wait_recv()
+        send_right(slots.at[chunk], chunk).wait_recv()
 
         @pl.when(chunk + 2 < count_right)
         def _():
-            send_right(from_left.at[chunk], chunk + 2).start()
+            send_right(slots.at[chunk], chunk + 2).start()
 
     def pass_left(chunk):
-        send_left(from_right.at[chunk], chunk).wait_recv()
+        send_left(slots.at[offset + chunk], chunk).wait_recv()
 
         @pl.when(chunk + 2 < count_left)
         def _():
-            send_left(from_right.at[chunk], chunk + 2).start()
+            send_left(slots.at[offset + chunk], chunk + 2).start()
 
     barrier = pltpu.get_barrier_semaphore()
     for neighbour in (right, left):
@@ -114,7 +124,11 @@
     loads = (
         pltpu.make_async_copy(hist_hbm, own, load_sem.at[0]),
         pltpu.make_async_copy(cand_hbm, cand, load_sem.at[1]),
-        pltpu.make_async_copy(w_in_hbm, w_in, load_sem.at[2]),
+        pltpu.make_async_copy(gain_in_hbm, gain_in_ref, load_sem.at[2]),
+        pltpu.make_async_copy(gain_attn_hbm, gain_attn_ref, load_sem.at[3]),
+        pltpu.make_async_copy(len_hbm, len_ref, load_sem.at[4]),
+        pltpu.make_async_copy(assign_hbm, assign_ref, load_sem.at[5]),
+        pltpu.make_async_copy(w_in_hbm, w_in, load_sem.at[6]),
     )
     for load in loads:
         load.start()
@@ -124,6 +138,8 @@
         send_right(own.at[chunk], chunk).start()
         send_left(own.at[hist_local - 1 - chunk], chunk).start()
 
+    for load in loads[1:6]:
+        load.wait()
     gain_in = gain_in_ref[...]
     lane = lax.broadcasted_iota(jnp.int32, (1, PAIR), 1)
     first_head = lane < HD
@@ -192,9 +208,8 @@
         xn[member * tok : (member + 1) * tok, :] = normed_rows(own[member], gain_in).astype(
             jnp.bfloat16
         )
-    loads[1].wait()
     xn[hist_rows:, :] = normed_rows(cand[...], gain_in).astype(jnp.bfloat16)
-    loads[2].wait()
+    loads[6].wait()
     for block in range(width // 256):
         cols = slice(block * 256, (block + 1) * 256)
         part = 0.5 * jnp.dot(xn[...], w_in[:, cols], preferred_element_type=jnp.float32)
@@ -220,16 +235,16 @@
         attend_rows(member, member, me, 0, tok, True)
 
     def unit(first, first_member, first_block, second, second_member, second_block):
-        for side, chunk in enumerate((first, second)):
-            xn[side * tok : (side + 1) * tok, :] = normed_rows(chunk[...], gain_in).astype(
+        for side, slot in enumerate((first, second)):
+            xn[side * tok : (side + 1) * tok, :] = normed_rows(slots[slot], gain_in).astype(
                 jnp.bfloat16
             )
         project_keys()
         attend(first_member, 0, first_block)
         attend(second_member, 1, second_block)
 
-    def block_right(chunk):
-        return lax.rem(me + 1 + lax.div(chunk, 2), ring)
+    def block_at(way, chunk):
+        return lax.rem(me + ring + way * (1 + lax.div(chunk, 2)), ring)
 
     @pl.loop(0, lead)
     def _(chunk):
@@ -237,7 +252,7 @@
 
     @pl.loop(0, turns)
     def _(turn):
-        @pl.when(turn + lead < base + extra)
+        @pl.when((turn + lead < base + extra) & ((late == 0) | (turn < turns - 2)))
         def _():
             pass_left(turn + lead)
 
@@ -245,32 +260,45 @@
         other = turn + 2 * jnp.minimum(early, lax.div(jnp.maximum(turn - 1, 0), 2))
         member = lax.rem(turn, 2)
         unit(
-            from_left.at[turn],
+            turn,
             member,
-            lax.rem(me + ring - 1 - lax.div(turn, 2), ring),
-            from_right.at[other],
+            block_at(-1, turn),
+            offset + other,
             lax.rem(other + 1, 2),
-            block_right(other),
-        )
-
-        due_late = (late > 0) & ((turn == turns - 4) | (turn == turns - 2))
+            block_at(1, other),
+        )
+
+        due_first, due_last = (late > 0) & (turn == turns - 3), (late > 0) & (turn == turns - 2)
         due_early = ((early > 0) & (turn == 2)) | ((early > 1) & (turn == 4))
-        chunk = turn + 2 * late + (turn - 1) * jnp.minimum(me, 1)
-
-        @pl.when(due_late)
-        def _():
-            pass_left(chunk)
-            pass_left(chunk + 1)
-
-        @pl.when(due_late | due_early)
-        def _():
+        due_back = (back > 0) & (turn == turns - 1)
+        chunk = 2 * turn - 1 + (7 - turns) * (1 - jnp.minimum(me, 1))
+        chunk = (1 - back) * chunk + back * (turn + 1)
+
+        @pl.when(due_first)
+        def _():
+            for ahead in range(1, 5):
+                pass_left(turn + ahead)
+
+        @pl.when(due_last)
+        def _():
+            for ahead in range(4, 6):
+                pass_left(turn + ahead)
+
+        @pl.when(due_back)
+        def _():
+            for ahead in range(1, 3):
+                pass_right(turn + ahead)
+
+        @pl.when(due_first | due_last | due_early | due_back)
+        def _():
+            slot = chunk + offset * (1 - back)
             unit(
-                from_right.at[chunk],
-                lax.rem(chunk + 1, 2),
-                block_right(chunk),
-                from_right.at[chunk + 1],
-                lax.rem(chunk, 2),
-                block_right(chunk + 1),
+                slot,
+                lax.rem(chunk + 1 - back, 2),
+                block_at(1 - 2 * back, chunk),
+                slot + 1,
+                lax.rem(chunk + back, 2),
+                block_at(1 - 2 * back, chunk + 1),
             )
 
     gain_attn = gain_attn_ref[...]
@@ -279,10 +307,19 @@
         attended = attended.astype(jnp.bfloat16)
         return (normed_rows(attended, gain_attn) * gates.astype(jnp.float32)).astype(jnp.bfloat16)
 
+    def store(first_row, last_row, number):
+        there = pl.ds(first_row, last_row - first_row)
+        return pltpu.make_async_copy(
+            gated_rows.at[there], gated_hbm.at[there], store_sem.at[number]
+        )
+
+    stores = []
     for member in range(hist_local):
         mine = slice(member * tok, (member + 1) * tok)
         attended = jnp.concatenate([acc[member, pair, :tok, :] for pair in range(pairs)], axis=1)
-        gated_out[mine, :] = gated(attended, gate[mine, :])
+        gated_rows[mine, :] = gated(attended, gate[mine, :])
+        stores.append(store(mine.start, mine.stop, member))
+        stores[-1].start()
     crossed = jnp.concatenate(
         [
             sum(acc[member, pair, tok:, :] for member in range(hist_local))
@@ -290,7 +327,9 @@
         ],
         axis=1,
     )
-    gated_out[hist_rows:, :] = gated(crossed, gate[hist_rows:, :])
+    gated_rows[hist_rows:, :] = gated(crossed, gate[hist_rows:, :])
+    stores.append(store(hist_rows, hist_rows + cands, hist_local))
+    stores[-1].start()
 
     @pl.loop(0, count_right)
     def _(chunk):
@@ -299,6 +338,9 @@
     @pl.loop(0, count_left)
     def _(chunk):
         send_left(own.at[0], chunk).wait_send()
+
+    for copy in stores:
+        copy.wait()
 
 
 def output_kernel(gated, w_out, history, candidates, history_out, candidate_out):
@@ -325,19 +367,22 @@
     all_rows = hist_local * tok + cands
     pairs = width // PAIR
     whole = pl.BlockSpec(memory_space=pltpu.VMEM)
-    scalars = pl.BlockSpec(memory_space=pltpu.SMEM)
     there = pl.BlockSpec(memory_space=pltpu.HBM)
     gated = pl.pallas_call(
         functools.partial(attend_kernel, ring),
         out_shape=jax.ShapeDtypeStruct((all_rows, width), jnp.bfloat16),
-        in_specs=[there, there, scalars, whole, there, whole, whole],
-        out_specs=whole,
+        in_specs=[there] * 7,
+        out_specs=there,
         scratch_shapes=[
-            pltpu.VMEM((ring - 1, tok, width), jnp.bfloat16),
-            pltpu.VMEM((ring - 1 + MOST_EXTRA, tok, width), jnp.bfloat16),
+            pltpu.VMEM((2 * (ring - 1 + MOST_EXTRA), tok, width), jnp.bfloat16),
             pltpu.VMEM((hist_local, tok, width), jnp.bfloat16),
             pltpu.VMEM((cands, width), jnp.bfloat16),
+            pltpu.SMEM(lengths.shape, jnp.int32),
+            pltpu.VMEM(assignment.shape, jnp.int32),
             pltpu.VMEM(weight_in.shape, jnp.bfloat16),
+            pltpu.VMEM((1, width), jnp.float32),
+            pltpu.VMEM((1, width), jnp.float32),
+            pltpu.VMEM((all_rows, width), jnp.bfloat16),
             pltpu.VMEM((all_rows, width), jnp.bfloat16),
             pltpu.VMEM((all_rows, width), jnp.bfloat16),
             pltpu.VMEM((hist_local, pairs, 2 * rows, PAIR), jnp.bfloat16),
@@ -345,9 +390,10 @@
             pltpu.VMEM((hist_local, pairs, rows, PAIR), jnp.float32),
             pltpu.VMEM((hist_local, rows, PAIR), jnp.float32),
             pltpu.VMEM((rows, PAIR), jnp.float32),
-            pltpu.SemaphoreType.DMA((3,)),
-            pltpu.SemaphoreType.DMA((ring - 1,)),
-            pltpu.SemaphoreType.DMA((ring - 1,)),
+            pltpu.SemaphoreType.DMA((7,)),
+            pltpu.SemaphoreType.DMA((hist_local + 1,)),
+            pltpu.SemaphoreType.DMA((ring - 1 + MOST_EXTRA,)),
+            pltpu.SemaphoreType.DMA((ring - 1 + MOST_EXTRA,)),
             pltpu.SemaphoreType.DMA((ring - 1 + MOST_EXTRA,)),
             pltpu.SemaphoreType.DMA((ring - 1 + MOST_EXTRA,)),
         ],

time: 161 us -> 155 us (0.963)
  Pallas kernels: 158 us -> 153 us
    pallas_call x1, Pallas kernels: 157 us -> 152 us  [per_device(): pl.pallas_call(functools.partial(attend_kernel, ring), out_shape=jax.Shap...]
where the time goes in v2:
time: 155 us
  Pallas kernels  153 us (99%)
    pallas_call x1, Pallas kernels, per_device(): pl.pallas_call(functools.partial(attend_kernel, ring), out_shape=jax.Shap...  152 us

profile of v2, /device:TPU:46, one launch (start us, length us, event | category | flops | bytes accessed | tf_op | source)
XLA Modules:
  0.0 155.1 jit_solution(8158233003982237516)
XLA Ops:
  0.6 0.0 copy-start.2
  0.6 0.0 copy-start
  0.7 0.0 copy-start.3
  0.7 151.8 %shard_map.95.gated = bf16[256,1024]{1,0:T(8,128)(2,1)} custom-call(bf16[2,96,1024]{2,1,0:T(8,128)(2,1)} %history.1, bf16[64,1024]{1,0:T(8,128)(2,1)} %bitcast.4, s32[2]{0:T(128)} %len_hbm.1, s32[1,64]{1,0:T(1,128)} %assign_hbm.1, bf16[1024,4096]{1,0:T(8,128)(2,1)} %w_in_hbm.1, f32[1,1024]{1,0:T(1,128)} %bitcast.6, f32[1,1024]{1,0:T(1,128)} %bitcast.7), custom_call_target="tpu_custom_call" | custom-call | tf_op jit(solution)/shard_map/pallas_call | solution.py:371
  152.5 0.0 copy-done.2
  152.5 0.0 copy-done
  152.5 0.0 copy-done.3
  152.5 0.0 copy-start.1
  152.6 1.0 copy-done.1
  153.6 1.5 shard_map.96
Async XLA Ops:
  0.6 151.9 %copy-start.2 = (bf16[2,96,1024]{2,1,0:T(8,128)(2,1)S(1)}, bf16[2,96,1024]{2,1,0:T(8,128)(2,1)}, u32[]{:S(2)}) copy-start(bf16[2,96,1024]{2,1,0:T(8,128)(2,1)} %history.1) | copy-start | bytes 1179652
  0.6 151.9 %copy-start = (bf16[1024,1024]{1,0:T(8,128)(2,1)S(1)}, bf16[1024,1024]{1,0:T(8,128)(2,1)}, u32[]{:S(2)}) copy-start(bf16[1024,1024]{1,0:T(8,128)(2,1)} %w_out.1) | copy-start | bytes 6291460
  0.7 151.9 %copy-start.3 = (bf16[1,64,1024]{2,1,0:T(8,128)(2,1)S(1)}, bf16[1,64,1024]{2,1,0:T(8,128)(2,1)}, u32[]{:S(2)}) copy-start(bf16[1,64,1024]{2,1,0:T(8,128)(2,1)} %param.9) | copy-start | bytes 393220
  152.5 1.0 copy-start.1

commit v3 on v2

--- a/solution.py
+++ b/solution.py
@@ -45,7 +45,7 @@
     w_in_hbm,
     gain_in_hbm,
     gain_attn_hbm,
-    gated_hbm,
+    gated_out,
     slots,
     own,
     cand,
@@ -54,7 +54,6 @@
     w_in,
     gain_in_ref,
     gain_attn_ref,
-    gated_rows,
     xn,
     gate,
     qz,
@@ -63,7 +62,6 @@
     lim,
     mask,
     load_sem,
-    store_sem,
     right_send,
     right_recv,
     left_send,
@@ -307,19 +305,10 @@
         attended = attended.astype(jnp.bfloat16)
         return (normed_rows(attended, gain_attn) * gates.astype(jnp.float32)).astype(jnp.bfloat16)
 
-    def store(first_row, last_row, number):
-        there = pl.ds(first_row, last_row - first_row)
-        return pltpu.make_async_copy(
-            gated_rows.at[there], gated_hbm.at[there], store_sem.at[number]
-        )
-
-    stores = []
     for member in range(hist_local):
         mine = slice(member * tok, (member + 1) * tok)
         attended = jnp.concatenate([acc[member, pair, :tok, :] for pair in range(pairs)], axis=1)
-        gated_rows[mine, :] = gated(attended, gate[mine, :])
-        stores.append(store(mine.start, mine.stop, member))
-        stores[-1].start()
+        gated_out[mine, :] = gated(attended, gate[mine, :])
     crossed = jnp.concatenate(
         [
             sum(acc[member, pair, tok:, :] for member in range(hist_local))
@@ -327,9 +316,7 @@
         ],
         axis=1,
     )
-    gated_rows[hist_rows:, :] = gated(crossed, gate[hist_rows:, :])
-    stores.append(store(hist_rows, hist_rows + cands, hist_local))
-    stores[-1].start()
+    gated_out[hist_rows:, :] = gated(crossed, gate[hist_rows:, :])
 
     @pl.loop(0, count_right)
     def _(chunk):
@@ -338,9 +325,6 @@
     @pl.loop(0, count_left)
     def _(chunk):
         send_left(own.at[0], chunk).wait_send()
-
-    for copy in stores:
-        copy.wait()
 
 
 def output_kernel(gated, w_out, history, candidates, history_out, candidate_out):
@@ -370,9 +354,9 @@
     there = pl.BlockSpec(memory_space=pltpu.HBM)
     gated = pl.pallas_call(
         functools.partial(attend_kernel, ring),
-        out_shape=jax.ShapeDtypeStruct((all_rows, width), jnp.bfloat16),
+        out_shape=pltpu.VMEM((all_rows, width), jnp.bfloat16),
         in_specs=[there] * 7,
-        out_specs=there,
+        out_specs=whole,
         scratch_shapes=[
             pltpu.VMEM((2 * (ring - 1 + MOST_EXTRA), tok, width), jnp.bfloat16),
             pltpu.VMEM((hist_local, tok, width), jnp.bfloat16),
@@ -384,14 +368,12 @@
             pltpu.VMEM((1, width), jnp.float32),
             pltpu.VMEM((all_rows, width), jnp.bfloat16),
             pltpu.VMEM((all_rows, width), jnp.bfloat16),
-            pltpu.VMEM((all_rows, width), jnp.bfloat16),
             pltpu.VMEM((hist_local, pairs, 2 * rows, PAIR), jnp.bfloat16),
             pltpu.VMEM((2 * pairs, hist_local * tok, PAIR), jnp.bfloat16),
             pltpu.VMEM((hist_local, pairs, rows, PAIR), jnp.float32),
             pltpu.VMEM((hist_local, rows, PAIR), jnp.float32),
             pltpu.VMEM((rows, PAIR), jnp.float32),
             pltpu.SemaphoreType.DMA((7,)),
-            pltpu.SemaphoreType.DMA((hist_local + 1,)),
             pltpu.SemaphoreType.DMA((ring - 1 + MOST_EXTRA,)),
             pltpu.SemaphoreType.DMA((ring - 1 + MOST_EXTRA,)),
             pltpu.SemaphoreType.DMA((ring - 1 + MOST_EXTRA,)),

time: 155 us -> 154 us (level)
  no operation moved by 1% of the time
where the time goes in v3:
time: 154 us
  Pallas kernels  153 us (99%)
    pallas_call x1, Pallas kernels, per_device(): pl.pallas_call(functools.partial(attend_kernel, ring), out_shape=pltpu.VM...  152 us

profile of v3, /device:TPU:46, one launch (start us, length us, event | category | flops | bytes accessed | tf_op | source)
XLA Modules:
  0.0 153.9 jit_solution(8132695494858965387)
XLA Ops:
  0.6 0.0 copy-start.1
  0.6 0.0 copy-start
  0.7 0.0 copy-start.2
  0.7 151.7 %shard_map.95.gated = bf16[256,1024]{1,0:T(8,128)(2,1)S(1)} custom-call(bf16[2,96,1024]{2,1,0:T(8,128)(2,1)} %history.1, bf16[64,1024]{1,0:T(8,128)(2,1)} %bitcast.4, s32[2]{0:T(128)} %len_hbm.1, s32[1,64]{1,0:T(1,128)} %assign_hbm.1, bf16[1024,4096]{1,0:T(8,128)(2,1)} %w_in_hbm.1, f32[1,1024]{1,0:T(1,128)} %bitcast.6, f32[1,1024]{1,0:T(1,128)} %bitcast.7), custom_call_target="tpu_custom_call" | custom-call | tf_op jit(solution)/shard_map/pallas_call | solution.py:355
  152.3 0.0 copy-done.1
  152.3 0.0 copy-done
  152.4 0.0 copy-done.2
  152.4 1.5 shard_map.96
Async XLA Ops:
  0.6 151.7 %copy-start.1 = (bf16[2,96,1024]{2,1,0:T(8,128)(2,1)S(1)}, bf16[2,96,1024]{2,1,0:T(8,128)(2,1)}, u32[]{:S(2)}) copy-start(bf16[2,96,1024]{2,1,0:T(8,128)(2,1)} %history.1) | copy-start | bytes 1179652
  0.6 151.7 %copy-start = (bf16[1024,1024]{1,0:T(8,128)(2,1)S(1)}, bf16[1024,1024]{1,0:T(8,128)(2,1)}, u32[]{:S(2)}) copy-start(bf16[1024,1024]{1,0:T(8,128)(2,1)} %w_out.1) | copy-start | bytes 6291460
  0.7 151.7 %copy-start.2 = (bf16[1,64,1024]{2,1,0:T(8,128)(2,1)S(1)}, bf16[1,64,1024]{2,1,0:T(8,128)(2,1)}, u32[]{:S(2)}) copy-start(bf16[1,64,1024]{2,1,0:T(8,128)(2,1)} %param.9) | copy-start | bytes 393220

commit v4 on v3

--- a/solution.py
+++ b/solution.py
@@ -128,10 +128,11 @@
         pltpu.make_async_copy(assign_hbm, assign_ref, load_sem.at[5]),
         pltpu.make_async_copy(w_in_hbm, w_in, load_sem.at[6]),
     )
-    for load in loads:
+    for load in loads[:6]:
         load.start()
+    loads[0].wait()
+    loads[6].start()
     pl.semaphore_wait(barrier, 2)
-    loads[0].wait()
     for chunk in range(hist_local):
         send_right(own.at[chunk], chunk).start()
         send_left(own.at[hist_local - 1 - chunk], chunk).start()

time: 154 us -> 154 us (level)
  no operation moved by 1% of the time
where the time goes in v4:
time: 154 us
  Pallas kernels  153 us (99%)
    pallas_call x1, Pallas kernels, per_device(): pl.pallas_call(functools.partial(attend_kernel, ring), out_shape=pltpu.VM...  152 us

profile of v4, /device:TPU:46, one launch (start us, length us, event | category | flops | bytes accessed | tf_op | source)
XLA Modules:
  0.0 153.8 jit_solution(7506459539430717090)
XLA Ops:
  0.6 0.0 copy-start.1
  0.6 0.0 copy-start
  0.7 0.0 copy-start.2
  0.7 151.7 %shard_map.95.gated = bf16[256,1024]{1,0:T(8,128)(2,1)S(1)} custom-call(bf16[2,96,1024]{2,1,0:T(8,128)(2,1)} %history.1, bf16[64,1024]{1,0:T(8,128)(2,1)} %bitcast.4, s32[2]{0:T(128)} %len_hbm.1, s32[1,64]{1,0:T(1,128)} %assign_hbm.1, bf16[1024,4096]{1,0:T(8,128)(2,1)} %w_in_hbm.1, f32[1,1024]{1,0:T(1,128)} %bitcast.6, f32[1,1024]{1,0:T(1,128)} %bitcast.7), custom_call_target="tpu_custom_call" | custom-call | tf_op jit(solution)/shard_map/pallas_call | solution.py:356
  152.3 0.0 copy-done.1
  152.3 0.0 copy-done
  152.4 0.0 copy-done.2
  152.4 1.5 shard_map.96
Async XLA Ops:
  0.6 151.7 %copy-start.1 = (bf16[2,96,1024]{2,1,0:T(8,128)(2,1)S(1)}, bf16[2,96,1024]{2,1,0:T(8,128)(2,1)}, u32[]{:S(2)}) copy-start(bf16[2,96,1024]{2,1,0:T(8,128)(2,1)} %history.1) | copy-start | bytes 1179652
  0.6 151.7 %copy-start = (bf16[1024,1024]{1,0:T(8,128)(2,1)S(1)}, bf16[1024,1024]{1,0:T(8,128)(2,1)}, u32[]{:S(2)}) copy-start(bf16[1024,1024]{1,0:T(8,128)(2,1)} %w_out.1) | copy-start | bytes 6291460
  0.7 151.7 %copy-start.2 = (bf16[1,64,1024]{2,1,0:T(8,128)(2,1)S(1)}, bf16[1,64,1024]{2,1,0:T(8,128)(2,1)}, u32[]{:S(2)}) copy-start(bf16[1,64,1024]{2,1,0:T(8,128)(2,1)} %param.9) | copy-start | bytes 393220
